TPU v7x, 32 devices: a whole 2x2x4 slice. The times are simulated.
32 devices in a mesh: dp: 8 (over z, x), sub: 4 (over y, core).
Axes of the slice: x: 2, y: 2, z: 4, core: 2. Of those that a mesh axis runs over, the one named last changes fastest.
Arguments:
- block_in: bfloat16 [32, 322, 1152], P(('dp', 'sub')), may hold values from -6 to 6
- long_skip: bfloat16 [32, 322, 1152], P(('dp', 'sub')), may hold values from -6 to 6
- lengths: int32 [32], P(('dp', 'sub')), may hold values from 192 to 320, as said below
- grad_out: bfloat16 [32, 322, 1152], P(('dp', 'sub')), may hold values from -6 to 6
- w_skip: bfloat16 [2654208], P(('dp', 'sub')), may hold values from -0.125 to 0.125
- w_qkv: bfloat16 [3981312], P(('dp', 'sub')), may hold values from -0.1875 to 0.1875
- w_out: bfloat16 [1327104], P(('dp', 'sub')), may hold values from -1.5 to 1.5
- w_up: bfloat16 [5308416], P(('dp', 'sub')), may hold values from -0.1875 to 0.1875
- w_down: bfloat16 [5308416], P(('dp', 'sub')), may hold values from -0.09375 to 0.09375
- norm_gains: float32 [2, 1152], replicated, may hold values from 0.5 to 1.5
- biases: float32 [9, 1152], replicated, may hold values from -3 to 3
Outputs:
- layer_out: bfloat16 [32, 322, 1152], P(('dp', 'sub'))
- grad_in: bfloat16 [32, 322, 1152], P(('dp', 'sub'))
- grad_skip: bfloat16 [32, 322, 1152], P(('dp', 'sub'))
- grad_w_skip: float32 [2654208], P(('dp', 'sub'))
- grad_w_qkv: float32 [3981312], P(('dp', 'sub'))
- grad_w_out: float32 [1327104], P(('dp', 'sub'))
- grad_w_up: float32 [5308416], P(('dp', 'sub'))
- grad_w_down: float32 [5308416], P(('dp', 'sub'))
- grad_gains: float32 [2, 1152], replicated
- grad_biases: float32 [9, 1152], replicated
Inputs may be any that keep to these rules, and one draw needn't show every extreme that they name: In each item, slots 0 and 1 hold its time and class tokens, slots 2 to lengths + 1 hold its patches, and the rest is padding; in every draw at least one item has 320 patches and one has 192.
All inputs are finite; a program needn't handle non-finite values.
Results may differ from a plain program's by a relative error of at most 0.014.
Values may be sent and summed in bfloat16 or wider, within the bound.
A program may use at most 320 MiB of HBM per device.

v0:
```python
import jax
import jax.numpy as jnp
from jax import lax
from jax.sharding import PartitionSpec as P

HEADS = 16
HD = 72
FF = 4608
norm_epsilon = 1e-05
masked_score = -1e30


def product(left_side, right_side):
    return jnp.dot(left_side, right_side, preferred_element_type=jnp.float32)


def cross_rows(left_side, right_side):
    return lax.dot_general(
        left_side, right_side, (((0,), (0,)), ((), ())), preferred_element_type=jnp.float32
    )


def cross_cols(left_side, right_side):
    return lax.dot_general(
        left_side, right_side, (((1,), (1,)), ((), ())), preferred_element_type=jnp.float32
    )


def flat_rows(left_side, right_side):
    block = cross_rows(left_side, right_side).reshape(-1)
    return block


def norm_forward(stream, gain_row, shift_row):
    centred = stream - jnp.mean(stream, -1, keepdims=True)
    inverse = lax.rsqrt(jnp.mean(centred * centred, -1, keepdims=True) + norm_epsilon)
    normal = centred * inverse
    return (normal * gain_row + shift_row, normal, inverse)


def norm_backward(incoming, normal, inverse, gain_row):
    grad_gain = jnp.sum(incoming * normal, 0)
    grad_shift = jnp.sum(incoming, 0)
    scaled = incoming * gain_row
    centred = scaled - jnp.mean(scaled, -1, keepdims=True)
    grad_value = inverse * (centred - normal * jnp.mean(scaled * normal, -1, keepdims=True))
    return (grad_value, grad_gain, grad_shift)


def gelu_slope(hidden):
    cumulative = 0.5 * (1.0 + lax.erf(hidden * 0.5**0.5))
    density = jnp.exp(-0.5 * hidden * hidden) * (2.0 * jnp.pi) ** (-0.5)
    return cumulative + hidden * density


def attention_shares(queries, key_rows, key_valid, score_scale):
    scores = (
        jnp.einsum("ishd,ithd->ihst", queries, key_rows, preferred_element_type=jnp.float32)
        * score_scale
    )
    scores = jnp.where(key_valid[:, None, None, :], scores, masked_score)
    highest = jnp.max(scores, -1, keepdims=True)
    raised = jnp.exp(scores - highest)
    return raised / jnp.sum(raised, -1, keepdims=True)


def on_device(
    block_in, long_skip, lengths, grad_out, w_skip, w_qkv, w_out, w_up, w_down, norm_gains, biases
):
    item_count, slot_count, model_width = block_in.shape
    row_count = item_count * slot_count
    head_count = HEADS
    head_size = HD
    hidden_width = FF
    score_scale = HD ** (-0.5)
    key_valid = jnp.arange(slot_count, dtype=jnp.int32)[None, :] < lengths[:, None] + 2
    skip_full = lax.all_gather(w_skip, ("dp", "sub"), axis=0, tiled=True).reshape(
        2 * model_width, model_width
    )
    joined = jnp.concatenate([block_in, long_skip], -1).reshape(row_count, 2 * model_width)
    stream_one = product(joined, skip_full) + biases[0]
    normed, normal_one, inverse_one = norm_forward(stream_one, norm_gains[0], biases[1])
    normed_low = normed.astype(jnp.bfloat16)
    qkv_flat, out_flat = (
        lax.all_gather(w_qkv, ("dp", "sub"), axis=0, tiled=True),
        lax.all_gather(w_out, ("dp", "sub"), axis=0, tiled=True),
    )
    qkv_full = qkv_flat.reshape(model_width, 3 * model_width)
    out_full = out_flat.reshape(model_width, model_width)
    triple = product(normed_low, qkv_full).astype(jnp.bfloat16)
    triple = triple.reshape(item_count, slot_count, 3, head_count, head_size)
    queries = triple[:, :, 0]
    key_rows = triple[:, :, 1]
    values = triple[:, :, 2]
    shares = attention_shares(queries, key_rows, key_valid, score_scale)
    shares_low = shares.astype(jnp.bfloat16)
    mixture = jnp.einsum("ihst,ithd->ishd", shares_low, values, preferred_element_type=jnp.float32)
    mixture_low = mixture.reshape(row_count, model_width).astype(jnp.bfloat16)
    stream_two = stream_one + (product(mixture_low, out_full) + biases[2])
    up_flat, down_flat = (
        lax.all_gather(w_up, ("dp", "sub"), axis=0, tiled=True),
        lax.all_gather(w_down, ("dp", "sub"), axis=0, tiled=True),
    )
    up_full = up_flat.reshape(model_width, hidden_width)
    down_full = down_flat.reshape(hidden_width, model_width)
    normed_two, normal_two, inverse_two = norm_forward(stream_two, norm_gains[1], biases[3])
    normed_two_low = normed_two.astype(jnp.bfloat16)
    hidden = product(normed_two_low, up_full) + biases[4:8].reshape(hidden_width)
    active_low = jax.nn.gelu(hidden, approximate=False).astype(jnp.bfloat16)
    result = stream_two + (product(active_low, down_full) + biases[8])
    layer_out = result.astype(jnp.bfloat16).reshape(item_count, slot_count, model_width)
    row_mask = key_valid.reshape(row_count, 1).astype(jnp.float32)
    start_grad = grad_out.reshape(row_count, model_width).astype(jnp.float32) * row_mask
    up_again, down_again = (
        lax.all_gather(w_up, ("dp", "sub"), axis=0, tiled=True),
        lax.all_gather(w_down, ("dp", "sub"), axis=0, tiled=True),
    )
    up_back = up_again.reshape(model_width, hidden_width)
    down_back = down_again.reshape(hidden_width, model_width)
    grad_branch = start_grad.astype(jnp.bfloat16)
    bias_down = jnp.sum(grad_branch.astype(jnp.float32), 0)
    part_down = lax.psum_scatter(
        flat_rows(active_low, grad_branch), ("dp", "sub"), scatter_dimension=0, tiled=True
    )
    grad_active = cross_cols(grad_branch, down_back)
    grad_hidden = (grad_active * gelu_slope(hidden)).astype(jnp.bfloat16)
    bias_up = jnp.sum(grad_hidden.astype(jnp.float32), 0)
    part_up = lax.psum_scatter(
        flat_rows(normed_two_low, grad_hidden), ("dp", "sub"), scatter_dimension=0, tiled=True
    )
    grad_normed_two = cross_cols(grad_hidden, up_back)
    local_two, gain_two, shift_two = norm_backward(
        grad_normed_two, normal_two, inverse_two, norm_gains[1]
    )
    grad_two = start_grad + local_two
    qkv_again, out_again = (
        lax.all_gather(w_qkv, ("dp", "sub"), axis=0, tiled=True),
        lax.all_gather(w_out, ("dp", "sub"), axis=0, tiled=True),
    )
    qkv_back = qkv_again.reshape(model_width, 3 * model_width)
    out_back = out_again.reshape(model_width, model_width)
    grad_attn = grad_two.astype(jnp.bfloat16)
    bias_out = jnp.sum(grad_attn.astype(jnp.float32), 0)
    part_out = lax.psum_scatter(
        flat_rows(mixture_low, grad_attn), ("dp", "sub"), scatter_dimension=0, tiled=True
    )
    grad_mixture = cross_cols(grad_attn, out_back).astype(jnp.bfloat16)
    grad_mixture = grad_mixture.reshape(item_count, slot_count, head_count, head_size)
    grad_shares = jnp.einsum(
        "ishd,ithd->ihst", grad_mixture, values, preferred_element_type=jnp.float32
    )
    grad_scores = shares * (grad_shares - jnp.sum(shares * grad_shares, -1, keepdims=True))
    grad_scores_low = grad_scores.astype(jnp.bfloat16)
    grad_queries = (
        jnp.einsum("ihst,ithd->ishd", grad_scores_low, key_rows, preferred_element_type=jnp.float32)
        * score_scale
    )
    grad_keys = (
        jnp.einsum("ihst,ishd->ithd", grad_scores_low, queries, preferred_element_type=jnp.float32)
        * score_scale
    )
    grad_values = jnp.einsum(
        "ihst,ishd->ithd", shares_low, grad_mixture, preferred_element_type=jnp.float32
    )
    grad_triple = jnp.stack([grad_queries, grad_keys, grad_values], 2).astype(jnp.bfloat16)
    grad_triple = grad_triple.reshape(row_count, 3 * model_width)
    part_qkv = lax.psum_scatter(
        flat_rows(normed_low, grad_triple), ("dp", "sub"), scatter_dimension=0, tiled=True
    )
    grad_normed = cross_cols(grad_triple, qkv_back)
    local_one, gain_one, shift_one = norm_backward(
        grad_normed, normal_one, inverse_one, norm_gains[0]
    )
    grad_one = (grad_two + local_one).astype(jnp.bfloat16)
    skip_back = lax.all_gather(w_skip, ("dp", "sub"), axis=0, tiled=True).reshape(
        2 * model_width, model_width
    )
    bias_skip = jnp.sum(grad_one.astype(jnp.float32), 0)
    part_skip = lax.psum_scatter(
        flat_rows(joined, grad_one), ("dp", "sub"), scatter_dimension=0, tiled=True
    )
    grad_joined = cross_cols(grad_one, skip_back).reshape(item_count, slot_count, 2 * model_width)
    grad_in = grad_joined[:, :, :model_width].astype(jnp.bfloat16)
    grad_skip = grad_joined[:, :, model_width:].astype(jnp.bfloat16)
    gains_part = jnp.stack([gain_one, gain_two], 0)
    biases_part = jnp.concatenate(
        [
            jnp.stack([bias_skip, shift_one, bias_out, shift_two], 0),
            bias_up.reshape(4, model_width),
            bias_down[None, :],
        ],
        0,
    )
    grad_gains, grad_biases = lax.psum((gains_part, biases_part), ("dp", "sub"))
    return (
        layer_out,
        grad_in,
        grad_skip,
        part_skip,
        part_qkv,
        part_out,
        part_up,
        part_down,
        grad_gains,
        grad_biases,
    )


def solution(mesh):
    placed = (
        P(("dp", "sub"), None, None),
        P(("dp", "sub"), None, None),
        P(("dp", "sub")),
        P(("dp", "sub"), None, None),
        P(("dp", "sub")),
        P(("dp", "sub")),
        P(("dp", "sub")),
        P(("dp", "sub")),
        P(("dp", "sub")),
        P(),
        P(),
    )
    return jax.shard_map(
        on_device,
        mesh=mesh,
        in_specs=placed,
        out_specs=(
            P(("dp", "sub"), None, None),
            P(("dp", "sub"), None, None),
            P(("dp", "sub"), None, None),
            P(("dp", "sub")),
            P(("dp", "sub")),
            P(("dp", "sub")),
            P(("dp", "sub")),
            P(("dp", "sub")),
            P(),
            P(),
        ),
        check_vma=False,
    )
```

profile of v0, /device:TPU:0, one launch (start us, length us, event | category | flops | bytes accessed | tf_op | source)
XLA Modules:
  0.0 1773.4 jit_solution(16730782300148881002)
XLA Ops:
  7.2 1.6 reshape.302
  9.7 2.0 reshape.300
  16.8 62.9 %all-gather.16.cloned.1.call-done = bf16[32,1,41472]{2,1,0:T(2,128)(2,1)} async-done(((bf16[1,1,41472]{2,1,0:T(2,128)(2,1)}), bf16[32,1,41472]{2,1,0:T(2,128)(2,1)}) %all-gather.16.cloned.1.call-update) | async-done | bytes 2654224 | tf_op jit(solution)/shard_map/all_gather | solution.py:86
  79.7 47.1 %reduce.10 = bf16[32,41472]{1,0:T(8,128)(2,1)S(1)} reduce(bf16[32,1,41472]{2,1,0:T(2,128)(2,1)} %all-gather.16.cloned.1.call-done, bf16[]{:T(256)} %constant.109), dimensions={1}, to_apply=%all-gather.1.reduce_sub_computation | reduce | bytes 5308418 | tf_op jit(solution)/shard_map/all_gather | solution.py:86
  126.8 5.0 reshape.286
  131.8 14.8 all-gather.8.cloned.1.call-done
  146.6 10.8 reshape.280
  157.4 4.9 fusion.59
  162.6 96.6 %all-gather.14.cloned.1.call-done = bf16[32,1,124416]{2,1,0:T(2,128)(2,1)} async-done(((bf16[1,1,124416]{2,1,0:T(2,128)(2,1)}), bf16[32,1,124416]{2,1,0:T(2,128)(2,1)}) %all-gather.14.cloned.1.call-update) | async-done | bytes 7962640 | tf_op jit(solution)/shard_map/all_gather | solution.py:85
  259.2 167.7 %reduce.9 = bf16[32,124416]{1,0:T(8,128)(2,1)} reduce(bf16[32,1,124416]{2,1,0:T(2,128)(2,1)} %all-gather.14.cloned.1.call-done, bf16[]{:T(256)} %constant.109), dimensions={1}, to_apply=%all-gather.reduce_sub_computation | reduce | bytes 15925250 | tf_op jit(solution)/shard_map/all_gather | solution.py:85
  426.9 14.8 reshape.281
  441.7 8.0 convolution_convert_fusion
  449.7 4.6 copy.36
  454.3 3.0 fusion.41
  457.3 3.7 fusion.60
  461.0 3.1 fusion.36
  467.5 19.1 %reshape.287 = bf16[1152,4608]{1,0:T(8,128)(2,1)} reshape(bf16[5308416]{0:T(1024)(128)(2,1)} %all-gather.10.cloned.1.call-done) | data formatting | bytes 21233664 | tf_op jit(solution)/shard_map/reshape | solution.py:104
  486.5 20.9 %fusion.5 = (bf16[322,4608]{1,0:T(8,128)(2,1)}, f32[322,4608]{1,0:T(8,128)}) fusion(f32[4608]{0:T(1024)S(1)} %add.128, bf16[1152,4608]{1,0:T(8,128)(2,1)} %reshape.287, f32[322,1152]{1,0:T(8,128)S(1)} %get-tuple-element.44, f32[1152]{0:T(1024)S(1)} %get-tuple-element.19, f32[1152]{0:T(1024)S(1)} %get-tuple-element.23, f32[322]{0:T(512)S(1)} %add_rsqrt_fusion, ...), kind=kOutput, calls=%fused_computation.13 | convolution fusion | flops 3518403840 | bytes 21033488 | tf_op jit(solution)/shard_map/dot_general | solution.py:14
  507.5 20.4 %reshape.288 = bf16[4608,1152]{1,0:T(8,128)(2,1)} reshape(bf16[5308416]{0:T(1024)(128)(2,1)} %all-gather.12.cloned.1.call-done) | data formatting | bytes 21233664 | tf_op jit(solution)/shard_map/reshape | solution.py:105
  527.8 8.4 convert_reduce_fusion
  536.3 9.5 multiply_reduce_fusion.1
  547.8 2.2 convolution_convert_fusion.2
  550.0 2.6 copy.38
  552.6 5.9 fusion.29
  558.5 8.3 multiply_reduce_fusion
  566.8 6.7 multiply_convert_fusion
  573.5 2.7 multiply_bitcast_fusion
  576.2 2.3 multiply_bitcast_fusion.1
  579.1 4.1 multiply_reduce_fusion.2
  583.2 8.6 fusion.55
  591.8 3.9 fusion.49
  595.7 10.5 fusion.56
  607.7 5.7 fusion.39
  613.5 11.2 reshape.292
  624.6 16.7 reshape.293
  641.4 6.5 reshape.294
  647.9 20.9 %reshape.295 = f32[5308416]{0:T(1024)} reshape(f32[1152,4608]{1,0:T(8,128)} %fusion.56) | data formatting | bytes 42467328 | tf_op jit(solution)/shard_map/reshape | solution.py:30
  668.8 13.0 fusion.45
  681.9 22.0 %reshape.296 = f32[5308416]{0:T(1024)} reshape(f32[4608,1152]{1,0:T(8,128)} %fusion.45) | data formatting | bytes 42467328 | tf_op jit(solution)/shard_map/reshape | solution.py:30
  704.1 42.0 %all-reduce.5 = (f32[2,1152]{1,0:T(2,128)}, f32[9,1152]{1,0:T(8,128)}) all-reduce(f32[2,1152]{1,0:T(2,128)S(1)} %pad_maximum_fusion, f32[9,1152]{1,0:T(8,128)S(1)} %concatenate.15), channel_id=1, replica_groups=mesh['dp'=8,'sub'=4] {'dp','sub'}, use_global_device_ids=true, to_apply=%region_18.19 | all-reduce | flops 12672 | bytes 101376 | tf_op jit(solution)/shard_map/psum | solution.py:194
  746.1 5.0 fusion.20
  752.4 8.2 fusion.24
  760.6 996.3 %all-reduce.9.cloned.1.call-done = (f32[2654208]{0:T(1024)}, f32[3981312]{0:T(1024)}, f32[1327104]{0:T(1024)}, f32[5308416]{0:T(1024)}, f32[5308416]{0:T(1024)}) async-done(((f32[2654208]{0:T(1024)}, f32[3981312]{0:T(1024)}, f32[1327104]{0:T(1024)}, f32[5308416]{0:T(1024)}, f32[5308416]{0:T(1024)}), (f32[2654208]{0:T(1024)}, f32[3981312]{0:T(1024)}, f32[1327104]{0:T(1024)}, f32[5308416]{0:T(1024)}, ...) | async-done | bytes 74317840
  1756.9 2.0 dynamic-slice.3
  1758.9 2.0 dynamic-slice.4
  1760.8 1.7 dynamic-slice
  1762.6 2.0 dynamic-slice.1
  1764.6 1.7 dynamic-slice.2
  (91 shorter events, 14.2 us)
Async XLA Ops:
  7.2 72.5 %all-gather.16.cloned.1.call-start = ((), (), s32[]{:S(2)}) async-start(), calls=%async_computation.4 | async-start | bytes 5474304 | tf_op jit(solution)/shard_map/all_gather | solution.py:86
  8.9 137.7 %all-gather.8.cloned.1.call-start = ((), (), s32[]{:S(2)}) async-start(), calls=%async_computation | async-start | bytes 5474304 | tf_op jit(solution)/shard_map/all_gather | solution.py:77
  9.6 249.6 %all-gather.14.cloned.1.call-start = ((), (), s32[]{:S(2)}) async-start(), calls=%async_computation.3 | async-start | bytes 16422912 | tf_op jit(solution)/shard_map/all_gather | solution.py:85
  11.7 455.7 %all-gather.10.cloned.1.call-start = ((), (), s32[]{:S(2)}) async-start(), calls=%async_computation.1 | async-start | bytes 10948608 | tf_op jit(solution)/shard_map/all_gather | solution.py:101
  12.3 495.2 %all-gather.12.cloned.1.call-start = ((), (), s32[]{:S(2)}) async-start(), calls=%async_computation.2 | async-start | bytes 10948608 | tf_op jit(solution)/shard_map/all_gather | solution.py:102
  12.9 1744.0 %all-reduce.9.cloned.1.call-start = ((), (), s32[]{:S(2)}) async-start(), calls=%async_computation.5 | async-start | bytes 148635648
  131.8 25.6 %copy-start.16 = (bf16[1,322,1152]{2,1,0:T(8,128)(2,1)S(1)}, bf16[1,322,1152]{2,1,0:T(8,128)(2,1)}, u32[]{:S(2)}) copy-start(bf16[1,322,1152]{2,1,0:T(8,128)(2,1)} %param.12) | copy-start | bytes 2225668
  131.8 25.6 %copy-start.18 = (bf16[1,322,1152]{2,1,0:T(8,128)(2,1)S(1)}, bf16[1,322,1152]{2,1,0:T(8,128)(2,1)}, u32[]{:S(2)}) copy-start(bf16[1,322,1152]{2,1,0:T(8,128)(2,1)} %param.11) | copy-start | bytes 2225668
  461.0 4.0 copy-start.2
  461.0 4.7 copy-start.10
  465.0 2.4 copy-start.12
  536.2 9.6 copy-start.6
  536.3 9.6 copy-start.8
  545.8 2.0 copy-start.11
  546.6 1.2 copy-start
  552.6 5.9 copy-start.14
  573.5 5.6 slice-start
  576.2 2.3 copy-start.15
  576.2 2.9 slice-start.1
  583.2 8.6 copy-start.1
  583.2 8.6 copy-start.13
  591.8 3.9 copy-start.7
  606.2 1.5 copy-start.17
  606.2 1.5 copy-start.19
  606.8 0.9 copy-start.4
  647.9 20.9 %copy-start.9 = (bf16[1,322,1152]{2,1,0:T(8,128)(2,1)S(1)}, bf16[1,322,1152]{2,1,0:T(8,128)(2,1)}, u32[]{:S(2)}) copy-start(bf16[1,322,1152]{2,1,0:T(8,128)(2,1)} %param.14) | copy-start | bytes 2225668
  703.8 42.3 %copy-start.5 = (bf16[322,1152]{1,0:T(8,128)(2,1)S(1)}, bf16[322,1152]{1,0:T(8,128)(2,1)}, u32[]{:S(2)}) copy-start(bf16[322,1152]{1,0:T(8,128)(2,1)} %copy-done.4) | copy-start | bytes 2225668
  746.1 6.3 copy-start.3
  746.1 6.3 copy-start.20
Sparse Core Ops, SparseCore 0:
  11.4 68.2 all-gather.15
  82.5 64.0 all-gather.7
  150.1 109.1 all-gather.13
  262.0 85.1 all-gather.9
  350.0 85.4 all-gather.11
  704.0 1052.8 all-reduce.8
where the time goes:
time: 1790 us; the launch traced here: 1770 us
  waiting for transfers between devices  1170 us (65%)
  other arithmetic  228 us (13%)
  local copies, waits for them, and re-layouts  176 us (10%)
  matrix products  140 us (8%)
  blocking collectives  42 us (2%)
    unnamed x7, waiting for transfers between devices  998 us
    all_gather x1, other arithmetic, on_device(): lax.all_gather(w_qkv, ('dp', 'sub'), axis=0, tiled=True)  168 us
    all_gather x1, waiting for transfers between devices, on_device(): lax.all_gather(w_qkv, ('dp', 'sub'), axis=0, tiled=True)  96.6 us
    reshape x5, local copies, waits for them, and re-layouts, flat_rows(): block = cross_rows(left_side, right_side).reshape(-1)  77.4 us
    all_gather x1, waiting for transfers between devices, on_device(): lax.all_gather(w_out, ('dp', 'sub'), axis=0, tiled=True)  62.9 us
    all_gather x1, other arithmetic, on_device(): lax.all_gather(w_out, ('dp', 'sub'), axis=0, tiled=True)  47.1 us
    dot_general x5, matrix products, product(): return jnp.dot(left_side, right_side, preferred_element_type=jnp.float32)  43.4 us
    psum x1, blocking collectives, on_device(): grad_gains, grad_biases = lax.psum((gains_part, biases_part), ('dp', 'sub'))  42 us
  transfers between devices with their start and end apart: 6, of which 4 were waited for; matrix products, arithmetic and copies ran while one was open for 19% of the time, Pallas kernels for 0%

commit v1 on v0

--- a/solution.py
+++ b/solution.py
@@ -8,6 +8,28 @@
 FF = 4608
 norm_epsilon = 1e-05
 masked_score = -1e30
+
+
+def in_order(blocks, dim):
+    blocks = jnp.moveaxis(blocks, 0, dim)
+    lengths = blocks.shape
+    return blocks.reshape(*lengths[:dim], lengths[dim] * lengths[dim + 1], *lengths[dim + 2 :])
+
+
+def doubled(x, axis):
+    count = lax.axis_size(axis)
+    blocks = x[None]
+    for level in range(count.bit_length() - 1):
+        apart = 1 << level
+        received = lax.ppermute(blocks, axis, [(i, i ^ apart) for i in range(count)])
+        both = jnp.stack([blocks, received])
+        upper = lax.axis_index(axis) >> level & 1
+        blocks = jnp.where(upper == 0, both, both[::-1]).reshape(-1, *x.shape)
+    return blocks
+
+
+def doubled_up(x, axis, dim):
+    return in_order(doubled(x, axis), dim)
 
 
 def product(left_side, right_side):
@@ -82,7 +104,7 @@
     normed, normal_one, inverse_one = norm_forward(stream_one, norm_gains[0], biases[1])
     normed_low = normed.astype(jnp.bfloat16)
     qkv_flat, out_flat = (
-        lax.all_gather(w_qkv, ("dp", "sub"), axis=0, tiled=True),
+        doubled_up(w_qkv, ("dp", "sub"), 0),
         lax.all_gather(w_out, ("dp", "sub"), axis=0, tiled=True),
     )
     qkv_full = qkv_flat.reshape(model_width, 3 * model_width)

time: 1790 us -> 1920 us (1.073)
  waiting for transfers between devices: 1170 us -> 1260 us
  other arithmetic: 228 us -> 252 us
    ppermute x0 -> x5, waiting for transfers between devices: none -> 240 us  [doubled(): lax.ppermute(blocks, axis, [(i, i ^ apart) for i in range(count)])]
    all_gather x1, waiting for transfers between devices: 96.6 us -> 23.6 us  [on_device(): lax.all_gather(w_qkv, ('dp', 'sub'), axis=0, tiled=True)]
    all_gather x1, waiting for transfers between devices: 62.9 us -> 0.01 us  [on_device(): lax.all_gather(w_out, ('dp', 'sub'), axis=0, tiled=True)]
  transfers between devices with their start and end apart: 6 -> 11, of which waited for: 4 -> 6; matrix products, arithmetic and copies ran while one was open for 19% -> 20% of each run, Pallas kernels for 0% -> 0%
where the time goes in v1:
time: 1920 us; the launch traced here: 1910 us
  waiting for transfers between devices  1260 us (66%)
  other arithmetic  252 us (13%)
  local copies, waits for them, and re-layouts  195 us (10%)
  matrix products  137 us (7%)
  blocking collectives  42 us (2%)
    unnamed x7, waiting for transfers between devices  996 us
    ppermute x5, waiting for transfers between devices, doubled(): lax.ppermute(blocks, axis, [(i, i ^ apart) for i in range(count)])  240 us
    all_gather x1, other arithmetic, on_device(): lax.all_gather(w_qkv, ('dp', 'sub'), axis=0, tiled=True)  168 us
    reshape x5, local copies, waits for them, and re-layouts, flat_rows(): block = cross_rows(left_side, right_side).reshape(-1)  77.5 us
    all_gather x1, other arithmetic, on_device(): lax.all_gather(w_out, ('dp', 'sub'), axis=0, tiled=True)  47.1 us
    psum x1, blocking collectives, on_device(): grad_gains, grad_biases = lax.psum((gains_part, biases_part), ('dp', 'sub'))  42 us
    dot_general x5, matrix products, cross_rows(): lax.dot_general(left_side, right_side, (((0,), (0,)), ((), ())), preferre...  41.6 us
    dot_general x5, matrix products, product(): return jnp.dot(left_side, right_side, preferred_element_type=jnp.float32)  40.6 us
  transfers between devices with their start and end apart: 11, of which 6 were waited for; matrix products, arithmetic and copies ran while one was open for 20% of the time, Pallas kernels for 0%

profile of v1, /device:TPU:0, one launch (start us, length us, event | category | flops | bytes accessed | tf_op | source)
XLA Modules:
  0.0 1910.8 jit_solution(17106814730526405482)
XLA Ops:
  15.7 2.6 collective-permute-start.1
  18.4 13.1 collective-permute-done.1
  36.3 26.6 %collective-permute-done.2 = bf16[4,124416]{1,0:T(4,128)(2,1)} collective-permute-done((bf16[4,124416]{1,0:T(4,128)(2,1)S(1)}, bf16[4,124416]{1,0:T(4,128)(2,1)}, u32[]{:S(2)}, u32[]{:S(2)}) %collective-permute-start.2) | collective-permute-done | bytes 995360 | tf_op jit(solution)/shard_map/ppermute | solution.py:24
  62.9 2.7 pad_maximum_fusion.2
  71.6 58.2 %collective-permute-done.3 = bf16[8,124416]{1,0:T(8,128)(2,1)} collective-permute-done((bf16[8,124416]{1,0:T(8,128)(2,1)}, bf16[8,124416]{1,0:T(8,128)(2,1)}, u32[]{:S(2)}, u32[]{:S(2)}) %collective-permute-start.3) | collective-permute-done | bytes 1990688 | tf_op jit(solution)/shard_map/ppermute | solution.py:24
  129.8 2.5 pad_maximum_fusion.1
  132.4 3.8 fusion.22
  136.2 2.6 collective-permute-start.4
  140.6 47.1 %reduce.9 = bf16[32,41472]{1,0:T(8,128)(2,1)S(1)} reduce(bf16[32,1,41472]{2,1,0:T(2,128)(2,1)} %all-gather.14.cloned.1.call-done, bf16[]{:T(256)} %constant.128), dimensions={1}, to_apply=%all-gather.reduce_sub_computation | reduce | bytes 5308418 | tf_op jit(solution)/shard_map/all_gather | solution.py:108
  187.7 5.0 reshape.300
  192.6 142.0 %collective-permute-done.4 = bf16[16,124416]{1,0:T(8,128)(2,1)} collective-permute-done((bf16[16,124416]{1,0:T(8,128)(2,1)}, bf16[16,124416]{1,0:T(8,128)(2,1)}, u32[]{:S(2)}, u32[]{:S(2)}) %collective-permute-start.4) | collective-permute-done | bytes 3981344 | tf_op jit(solution)/shard_map/ppermute | solution.py:24
  334.7 4.1 pad_maximum_fusion
  338.7 4.4 reverse_select_fusion
  343.2 14.8 reshape_reshape_reshape.3
  358.0 11.2 reshape.291
  369.1 5.2 fusion.61
  376.1 4.8 convolution_convert_fusion
  381.0 4.4 copy.42
  385.4 3.0 fusion.43
  388.4 3.7 fusion.62
  392.1 3.1 fusion.38
  398.5 23.6 %all-gather.16.cloned.1.call-done = bf16[32,1,124416]{2,1,0:T(2,128)(2,1)} async-done(((bf16[1,1,124416]{2,1,0:T(2,128)(2,1)}), bf16[32,1,124416]{2,1,0:T(2,128)(2,1)}) %all-gather.16.cloned.1.call-update) | async-done | bytes 7962640 | tf_op jit(solution)/shard_map/all_gather | solution.py:159
  422.1 167.8 %reduce.14 = bf16[32,124416]{1,0:T(8,128)(2,1)} reduce(bf16[32,1,124416]{2,1,0:T(2,128)(2,1)} %all-gather.16.cloned.1.call-done, bf16[]{:T(256)} %constant.128), dimensions={1}, to_apply=%all-gather.1.reduce_sub_computation | reduce | bytes 15925250 | tf_op jit(solution)/shard_map/all_gather | solution.py:159
  589.9 14.8 reshape.305
  604.8 19.1 reshape.301
  623.8 20.9 %fusion.5 = (bf16[322,4608]{1,0:T(8,128)(2,1)}, f32[322,4608]{1,0:T(8,128)}) fusion(f32[4608]{0:T(1024)S(1)} %add.136, bf16[1152,4608]{1,0:T(8,128)(2,1)} %reshape.301, f32[322,1152]{1,0:T(8,128)S(1)} %get-tuple-element.48, f32[1152]{0:T(1024)S(1)} %get-tuple-element.19, f32[1152]{0:T(1024)S(1)} %get-tuple-element.23, f32[322]{0:T(512)S(1)} %add_rsqrt_fusion, ...), kind=kOutput, calls=%fused_computation.15 | convolution fusion | flops 3518403840 | bytes 21033488 | tf_op jit(solution)/shard_map/dot_general | solution.py:36
  644.8 20.4 %reshape.302 = bf16[4608,1152]{1,0:T(8,128)(2,1)} reshape(bf16[5308416]{0:T(1024)(128)(2,1)} %all-gather.12.cloned.1.call-done) | data formatting | bytes 21233664 | tf_op jit(solution)/shard_map/reshape | solution.py:127
  665.1 8.4 convert_reduce_fusion
  673.6 9.5 multiply_reduce_fusion.1
  687.3 2.6 copy.44
  689.9 5.9 fusion.31
  695.8 8.3 multiply_reduce_fusion
  704.1 6.7 multiply_convert_fusion
  715.7 3.9 fusion.51
  719.6 10.5 fusion.58
  730.8 8.6 fusion.57
  739.4 4.2 multiply_reduce_fusion.2
  745.1 5.8 fusion.41
  750.9 11.2 reshape.307
  762.1 16.7 reshape.308
  778.8 6.5 reshape.309
  785.3 20.9 %reshape.310 = f32[5308416]{0:T(1024)} reshape(f32[1152,4608]{1,0:T(8,128)} %fusion.58) | data formatting | bytes 42467328 | tf_op jit(solution)/shard_map/reshape | solution.py:52
  806.3 12.8 fusion.47
  819.1 22.2 %reshape.311 = f32[5308416]{0:T(1024)} reshape(f32[4608,1152]{1,0:T(8,128)} %fusion.47) | data formatting | bytes 42467328 | tf_op jit(solution)/shard_map/reshape | solution.py:52
  841.5 42.0 %all-reduce.5 = (f32[2,1152]{1,0:T(2,128)}, f32[9,1152]{1,0:T(8,128)}) all-reduce(f32[2,1152]{1,0:T(2,128)S(1)} %pad_maximum_fusion.5, f32[9,1152]{1,0:T(8,128)S(1)} %concatenate.15), channel_id=1, replica_groups=mesh['dp'=8,'sub'=4] {'dp','sub'}, use_global_device_ids=true, to_apply=%region_18.19 | all-reduce | flops 12672 | bytes 101376 | tf_op jit(solution)/shard_map/psum | solution.py:216
  883.5 5.0 fusion.20
  889.8 8.2 fusion.26
  898.0 996.3 %all-reduce.9.cloned.1.call-done = (f32[2654208]{0:T(1024)}, f32[3981312]{0:T(1024)}, f32[1327104]{0:T(1024)}, f32[5308416]{0:T(1024)}, f32[5308416]{0:T(1024)}) async-done(((f32[2654208]{0:T(1024)}, f32[3981312]{0:T(1024)}, f32[1327104]{0:T(1024)}, f32[5308416]{0:T(1024)}, f32[5308416]{0:T(1024)}), (f32[2654208]{0:T(1024)}, f32[3981312]{0:T(1024)}, f32[1327104]{0:T(1024)}, f32[5308416]{0:T(1024)}, ...) | async-done | bytes 74317840
  (142 shorter events, 47.1 us)
Async XLA Ops:
  7.2 133.4 %all-gather.14.cloned.1.call-start = ((), (), s32[]{:S(2)}) async-start(), calls=%async_computation.3 | async-start | bytes 5474304 | tf_op jit(solution)/shard_map/all_gather | solution.py:108
  8.4 3.5 collective-permute-start
  10.7 347.3 %all-gather.8.cloned.1.call-start = ((), (), s32[]{:S(2)}) async-start(), calls=%async_computation | async-start | bytes 5474304 | tf_op jit(solution)/shard_map/all_gather | solution.py:99
  11.9 21.7 %copy-start.5 = (bf16[1,1,124416]{2,1,0:T(2,128)(2,1)}, bf16[1,1,124416]{2,1,0:T(2,128)(2,1)S(1)}, u32[]{:S(2)}) copy-start(bf16[1,1,124416]{2,1,0:T(2,128)(2,1)S(1)} %stack_broadcast_in_dim.3) | copy-start | bytes 746500
  15.7 15.8 collective-permute-start.1
  18.3 403.8 %all-gather.16.cloned.1.call-start = ((), (), s32[]{:S(2)}) async-start(), calls=%async_computation.4 | async-start | bytes 16422912 | tf_op jit(solution)/shard_map/all_gather | solution.py:159
  34.1 28.9 %collective-permute-start.2 = (bf16[4,124416]{1,0:T(4,128)(2,1)S(1)}, bf16[4,124416]{1,0:T(4,128)(2,1)}, u32[]{:S(2)}, u32[]{:S(2)}) collective-permute-start(bf16[4,124416]{1,0:T(4,128)(2,1)S(1)} %reshape.293), channel_id=1, source_target_pairs={{0,4},{1,5},{2,6},{3,7},{4,0},{5,1},{6,2},{7,3},{8,12},{9,13},{10,... | collective-permute-start | bytes 2985992 | tf_op jit(solution)/shard_map/ppermute | solution.py:24
  35.9 568.9 %all-gather.10.cloned.1.call-start = ((), (), s32[]{:S(2)}) async-start(), calls=%async_computation.1 | async-start | bytes 10948608 | tf_op jit(solution)/shard_map/all_gather | solution.py:123
  68.2 61.7 %collective-permute-start.3 = (bf16[8,124416]{1,0:T(8,128)(2,1)}, bf16[8,124416]{1,0:T(8,128)(2,1)}, u32[]{:S(2)}, u32[]{:S(2)}) collective-permute-start(bf16[8,124416]{1,0:T(8,128)(2,1)} %reshape.294), channel_id=1, source_target_pairs={{0,8},{1,9},{2,10},{3,11},{4,12},{5,13},{6,14},{7,15},{8,0},{9,1},... | collective-permute-start | bytes 5971976 | tf_op jit(solution)/shard_map/ppermute | solution.py:24
  69.8 575.0 %all-gather.12.cloned.1.call-start = ((), (), s32[]{:S(2)}) async-start(), calls=%async_computation.2 | async-start | bytes 10948608 | tf_op jit(solution)/shard_map/all_gather | solution.py:124
  132.4 7.4 copy-start.30
  132.4 7.5 copy-start.31
  136.2 198.4 %collective-permute-start.4 = (bf16[16,124416]{1,0:T(8,128)(2,1)}, bf16[16,124416]{1,0:T(8,128)(2,1)}, u32[]{:S(2)}, u32[]{:S(2)}) collective-permute-start(bf16[16,124416]{1,0:T(8,128)(2,1)} %get-tuple-element.37), channel_id=1, source_target_pairs={{0,16},{1,17},{2,18},{3,19},{4,20},{5,21},{6,22},{7,23},{8,24},{9,... | collective-permute-start | bytes 11943944 | tf_op jit(solution)/shard_map/ppermute | solution.py:24
  138.9 1755.4 %all-reduce.9.cloned.1.call-start = ((), (), s32[]{:S(2)}) async-start(), calls=%async_computation.5 | async-start | bytes 148635648
  139.9 234.7 %copy-start.22 = (f32[1152]{0:T(1024)}, f32[1152]{0:T(1024)S(1)}, u32[]{:S(2)}) copy-start(f32[1152]{0:T(1024)S(1)} %get-tuple-element.24) | copy-start | bytes 13828
  140.6 234.1 %copy-start.24 = (f32[1152]{0:T(1024)}, f32[1152]{0:T(1024)S(1)}, u32[]{:S(2)}) copy-start(f32[1152]{0:T(1024)S(1)} %get-tuple-element.21) | copy-start | bytes 13828
  357.9 11.2 copy-start.18
  358.0 11.2 copy-start.20
  369.1 7.0 copy-start.3
  374.3 6.6 copy-start.26
  374.7 6.3 copy-start.28
  392.1 4.0 copy-start.2
  392.1 4.7 copy-start.12
  396.1 2.4 copy-start.14
  673.5 9.5 copy-start.8
  673.6 9.6 copy-start.10
  683.1 2.0 copy-start.13
  683.9 1.2 copy-start
  689.9 5.9 copy-start.16
  713.3 2.3 copy-start.1
  713.3 2.3 copy-start.15
  715.6 3.9 copy-start.9
  719.6 10.5 copy-start.17
  730.1 0.7 copy-start.23
  730.1 0.7 copy-start.25
  730.1 0.7 copy-start.27
  730.1 0.7 copy-start.29
  730.1 9.3 slice-start
  730.8 8.6 slice-start.1
  743.6 1.5 copy-start.19
  743.6 1.5 copy-start.21
  744.2 0.9 copy-start.6
  785.3 20.9 %copy-start.11 = (bf16[1,322,1152]{2,1,0:T(8,128)(2,1)S(1)}, bf16[1,322,1152]{2,1,0:T(8,128)(2,1)}, u32[]{:S(2)}) copy-start(bf16[1,322,1152]{2,1,0:T(8,128)(2,1)} %param.14) | copy-start | bytes 2225668
  841.2 42.2 %copy-start.7 = (bf16[322,1152]{1,0:T(8,128)(2,1)S(1)}, bf16[322,1152]{1,0:T(8,128)(2,1)}, u32[]{:S(2)}) copy-start(bf16[322,1152]{1,0:T(8,128)(2,1)} %copy-done.6) | copy-start | bytes 2225668
  883.5 6.3 copy-start.4
  883.5 6.3 copy-start.32
Sparse Core Ops, SparseCore 0:
  11.4 74.9 all-gather.13
  89.2 158.8 all-gather.7
  251.6 170.5 all-gather.15
  424.9 85.1 all-gather.9
  512.8 85.4 all-gather.11
  841.4 1052.8 all-reduce.8
